TPU v7x, 32 devices: a whole 2x2x4 slice. The times are simulated.
32 devices in a mesh: dp: 4 (over x, core), tensor: 8 (over z, y).
Axes of the slice: x: 2, y: 2, z: 4, core: 2. Of those that a mesh axis runs over, the one named last changes fastest.
Arguments:
- attn_ctx: bfloat16 [2048, 8192], P('dp', 'tensor'), may hold values from -6 to 6
- w_out: bfloat16 [8192, 8192], P('tensor'), may hold values from -0.09375 to 0.09375
- resid: bfloat16 [2048, 8192], P(('dp', 'tensor')), may hold values from -6 to 6
- teacher_gain: bfloat16 [8192], replicated, may hold values from 0.25 to 1.75
- dest_row: int32 [2048], replicated, may hold values from 0 to 2047, as said below
- student_in: bfloat16 [2048, 4096], P('dp', 'tensor'), may hold values from -6 to 6
- student_gain: bfloat16 [4096], replicated, may hold values from 0.25 to 1.75
- w_gate: bfloat16 [4096, 14336], P('dp', 'tensor'), may hold values from -0.09375 to 0.09375
- w_up: bfloat16 [4096, 14336], P('dp', 'tensor'), may hold values from -0.09375 to 0.09375
- w_down: bfloat16 [14336, 4096], P('tensor', 'dp'), may hold values from -0.0625 to 0.0625
- proj: bfloat16 [4096, 8192], P('dp', 'tensor'), may hold values from -0.09375 to 0.09375
Outputs:
- student_out: bfloat16 [2048, 4096], P('dp', 'tensor')
- row_loss: float32 [2048], P('dp')
- residue: float32 [2048, 8192], P('dp', 'tensor')
Inputs may be any that keep to these rules, and one draw needn't show every extreme that they name: A permutation of the rows; of the 64 rows i in one aligned block of teacher rows, at most 32 have dest_row[i] in any one tile of 512 student rows, and some tile receives exactly 32 of them.
All inputs are finite; a program needn't handle non-finite values.
Results may differ from a plain program's by a relative error of at most 0.012.
Values may be sent and summed in bfloat16 or wider, within the bound.
A program may use at most 192 MiB of HBM per device.

v0:
```python
import jax
import jax.numpy as jnp
from jax import lax
from jax.sharding import PartitionSpec as P

HT = 8192


def local(
    attn_ctx,
    w_out,
    resid,
    teacher_gain,
    dest_row,
    student_in,
    student_gain,
    w_gate,
    w_up,
    w_down,
    proj,
):
    tensor_count = lax.axis_size("tensor")
    group_count = lax.axis_size("dp")
    tile_rows = attn_ctx.shape[0]
    own_rows = resid.shape[0]
    portion = attn_ctx
    summed = lax.psum_scatter(
        jnp.dot(portion, w_out, preferred_element_type=jnp.float32).astype(jnp.bfloat16),
        "tensor",
        scatter_dimension=0,
        tiled=True,
    ).astype(jnp.float32)
    teacher_hidden = resid.astype(jnp.float32) + summed
    square_mean = jnp.mean(teacher_hidden * teacher_hidden, axis=1, keepdims=True)
    teacher_final = (
        teacher_hidden * lax.rsqrt(square_mean + 1e-06) * teacher_gain.astype(jnp.float32)
    ).astype(jnp.bfloat16)
    capacity = 2 * own_rows // group_count
    source_count = group_count * tensor_count
    group_ids = (dest_row // tile_rows).reshape(source_count, own_rows)
    onehot = (group_ids[:, :, None] == jnp.arange(group_count)[None, None, :]).astype(jnp.int32)
    slot_index = jnp.sum((jnp.cumsum(onehot, 1) - onehot) * onehot, 2)
    my_source = lax.axis_index("dp") * tensor_count + lax.axis_index("tensor")
    own_groups = lax.dynamic_index_in_dim(group_ids, my_source, 0, keepdims=False)
    own_slots = lax.dynamic_index_in_dim(slot_index, my_source, 0, keepdims=False)
    target_slot = own_groups * capacity + own_slots
    selector = (target_slot[None, :] == jnp.arange(group_count * capacity)[:, None]).astype(
        jnp.bfloat16
    )
    packed = jnp.dot(selector, teacher_final, preferred_element_type=jnp.float32).astype(
        jnp.bfloat16
    )
    col_width = teacher_final.shape[1] // tensor_count
    send_blocks = packed.reshape(group_count, capacity, tensor_count, col_width).transpose(
        0, 2, 1, 3
    )
    arrived = lax.all_to_all(
        lax.all_to_all(send_blocks, "dp", split_axis=0, concat_axis=0, tiled=True),
        "tensor",
        split_axis=1,
        concat_axis=1,
        tiled=True,
    )
    flattened = arrived.reshape(source_count * capacity, col_width)
    arrival_index = (jnp.arange(source_count)[:, None] * capacity + slot_index).reshape(-1)
    inverse = jnp.zeros(dest_row.shape, jnp.int32).at[dest_row].set(arrival_index)
    own_arrivals = lax.dynamic_slice_in_dim(inverse, lax.axis_index("dp") * tile_rows, tile_rows, 0)
    target = jnp.take(flattened, own_arrivals, axis=0)
    gathered = lax.all_gather(student_in, "tensor", axis=1, tiled=True)
    x_full = gathered.astype(jnp.float32)
    student_mean = jnp.mean(x_full * x_full, axis=1, keepdims=True)
    normed = (x_full * lax.rsqrt(student_mean + 1e-05) * student_gain.astype(jnp.float32)).astype(
        jnp.bfloat16
    )

    def add_rows(portion):
        return jnp.dot(normed, portion, preferred_element_type=jnp.float32)

    gate_acts = add_rows(lax.all_gather(w_gate, "dp", axis=0, tiled=True))
    up_acts = add_rows(lax.all_gather(w_up, "dp", axis=0, tiled=True))
    hidden = (jax.nn.silu(gate_acts) * up_acts).astype(jnp.bfloat16)
    partial_sum = jnp.dot(
        hidden, lax.all_gather(w_down, "dp", axis=1, tiled=True), preferred_element_type=jnp.float32
    )
    local_cols = student_in.shape[1]
    mlp_sum = lax.psum(partial_sum.astype(jnp.bfloat16), "tensor").astype(jnp.float32)
    out_full = (x_full + mlp_sum).astype(jnp.bfloat16)
    out_local = lax.dynamic_slice_in_dim(
        out_full, lax.axis_index("tensor") * local_cols, local_cols, 1
    )
    pred = jnp.dot(
        out_full, lax.all_gather(proj, "dp", axis=0, tiled=True), preferred_element_type=jnp.float32
    )
    residue = pred - target.astype(jnp.float32)
    row_error = jnp.sum(residue * residue, axis=1)
    row_loss = lax.psum(row_error, "tensor") / HT
    return (out_local, row_loss, residue)


def solution(mesh):
    placed = (
        P("dp", "tensor"),
        P("tensor", None),
        P(("dp", "tensor"), None),
        P(),
        P(),
        P("dp", "tensor"),
        P(),
        P("dp", "tensor"),
        P("dp", "tensor"),
        P("tensor", "dp"),
        P("dp", "tensor"),
    )
    return jax.shard_map(
        local,
        mesh=mesh,
        in_specs=placed,
        out_specs=(P("dp", "tensor"), P("dp"), P("dp", "tensor")),
        check_vma=False,
    )
```

profile of v0, /device:TPU:0, one launch (start us, length us, event | category | flops | bytes accessed | tf_op | source)
XLA Modules:
  0.0 813.1 jit_solution(8429802727703756237)
XLA Ops:
  10.0 16.8 %convolution_convert_fusion = bf16[512,8192]{1,0:T(8,128)(2,1)} fusion(bf16[512,1024]{1,0:T(8,128)(2,1)S(1)} %copy-done, bf16[1024,8192]{1,0:T(8,128)(2,1)} %param.12), kind=kOutput, calls=%fused_computation.5 | convolution fusion | flops 8594128896 | bytes 26214400 | tf_op jit(solution)/shard_map/dot_general | solution.py:28
  27.5 59.9 %all-gather.6.cloned.1.call-done = bf16[512,4096]{1,0:T(8,128)(2,1)} async-done(((bf16[512,512]{1,0:T(8,128)(2,1)}), bf16[512,4096]{1,0:T(8,128)(2,1)}) %all-gather.6.cloned.1.call-update) | async-done | bytes 4194320 | tf_op jit(solution)/shard_map/all_gather | solution.py:69
  87.4 3.1 fusion
  90.5 90.7 %all-gather.8.cloned.1.call-done = bf16[4096,1792]{1,0:T(8,128)(2,1)} async-done(((bf16[1024,1792]{1,0:T(8,128)(2,1)}), bf16[4096,1792]{1,0:T(8,128)(2,1)}) %all-gather.8.cloned.1.call-update) | async-done | bytes 14680080 | tf_op jit(solution)/shard_map/all_gather | solution.py:79
  181.2 14.7 %fusion.11 = f32[512,1792]{1,0:T(8,128)} fusion(bf16[4096,1792]{1,0:T(8,128)(2,1)} %all-gather.8.cloned.1.call-done, bf16[512,4096]{1,0:T(8,128)(2,1)} %all-gather.6.cloned.1.call-done, f32[4096]{0:T(1024)S(1)} %convert_element_type.47, f32[512]{0:T(512)S(1)} %add_rsqrt_fusion), kind=kOutput, calls=%fused_computation.23 | convolution fusion | flops 7524581376 | bytes 22562816 | tf_op jit(solution)/shard_map/dot_general | solution.py:77
  195.8 80.9 %all-gather.12.cloned.1.call-done = bf16[1792,4096]{1,0:T(8,128)(2,1)} async-done(((bf16[1792,1024]{1,0:T(8,128)(2,1)}), bf16[1792,4096]{1,0:T(8,128)(2,1)}) %all-gather.12.cloned.1.call-update) | async-done | bytes 14680080 | tf_op jit(solution)/shard_map/all_gather | solution.py:83
  276.8 95.4 %all-gather.10.cloned.1.call-done = bf16[4096,1792]{1,0:T(8,128)(2,1)} async-done(((bf16[1024,1792]{1,0:T(8,128)(2,1)}), bf16[4096,1792]{1,0:T(8,128)(2,1)}) %all-gather.10.cloned.1.call-update) | async-done | bytes 14680080 | tf_op jit(solution)/shard_map/all_gather | solution.py:80
  372.2 28.8 %convolution_convert_fusion.2 = bf16[512,4096]{1,0:T(8,128)(2,1)} fusion(bf16[1792,4096]{1,0:T(8,128)(2,1)} %all-gather.12.cloned.1.call-done, f32[512,1792]{1,0:T(8,128)} %fusion.11, bf16[4096,1792]{1,0:T(8,128)(2,1)} %all-gather.10.cloned.1.call-done, bf16[512,4096]{1,0:T(8,128)(2,1)} %all-gather.6.cloned.1.call-done, f32[4096]{0:T(1024)S(1)} %convert_element_type.47, ...), kind=kOutput, calls=%fused_computation.11 | convolution fusion | flops 15048376320 | bytes 41437184 | tf_op jit(solution)/shard_map/dot_general | solution.py:82
  402.0 1.7 select_reduce_fusion
  403.9 119.3 %reduce-scatter.2.cloned.1.call-done = bf16[64,8192]{1,0:T(8,128)(2,1)} async-done(((bf16[512,8192]{1,0:T(8,128)(2,1)}), bf16[64,8192]{1,0:T(8,128)(2,1)}) %reduce-scatter.2.cloned.1.call-update) | async-done | bytes 1048592 | tf_op jit(solution)/shard_map/reduce_scatter | solution.py:27
  523.2 1.7 multiply_reduce_fusion.1
  524.9 2.0 convolution_convert_fusion.1
  529.5 28.2 %all_to_all.10 = bf16[4,8,32,1024]{3,2,1,0:T(8,128)(2,1)S(1)} all-to-all(bf16[4,8,32,1024]{3,2,1,0:T(8,128)(2,1)S(1)} %bitcast.17), channel_id=1, replica_groups=mesh['dp'=4,'tensor'=8] {'dp'}, dimensions={0} | all-to-all | bytes 4194304 | tf_op jit(solution)/shard_map/all_to_all | solution.py:58
  559.1 4.3 all-to-all-start.1
  563.7 8.3 %scatter_custom_fusion = s32[2048]{0:T(1024)S(1)} fusion(s32[2048]{0:T(1024)S(1)} %get-tuple-element.5, s32[2048]{0:T(1024)S(1)} %reshape.60, s32[]{:T(128)} %constant.62.clone.1), kind=kCustom, calls=%fused_computation.43 | custom fusion | bytes 8196 | tf_op jit(solution)/shard_map/scatter | solution.py:66
  572.1 64.3 %all-to-all-done.1 = bf16[4,8,32,1024]{3,2,0,1:T(8,128)(2,1)} async-done(((bf16[4,8,32,1024]{3,2,0,1:T(8,128)(2,1)}), bf16[4,8,32,1024]{3,2,0,1:T(8,128)(2,1)}, u32[]{:S(2)}, u32[]{:S(2)}) %all-to-all-start.1) | async-done | bytes 2097184 | tf_op jit(solution)/shard_map/all_to_all | solution.py:57
  636.5 1.8 copy.34
  638.3 2.8 gather_fusion
  641.1 73.8 %all-reduce.2.cloned.1.call-done = bf16[512,4096]{1,0:T(8,128)(2,1)} async-done(((bf16[512,4096]{1,0:T(8,128)(2,1)}), bf16[512,4096]{1,0:T(8,128)(2,1)}) %all-reduce.2.cloned.1.call-update) | async-done | bytes 4194320 | tf_op jit(solution)/shard_map/psum | solution.py:86
  714.9 5.0 fusion.3
  719.9 1.9 copy-done.2
  722.7 51.0 %all-gather.14.cloned.1.call-done = bf16[4096,1024]{1,0:T(8,128)(2,1)} async-done(((bf16[1024,1024]{1,0:T(8,128)(2,1)}), bf16[4096,1024]{1,0:T(8,128)(2,1)}) %all-gather.14.cloned.1.call-update) | async-done | bytes 8388624 | tf_op jit(solution)/shard_map/all_gather | solution.py:92
  773.7 10.6 %multiply_reduce_fusion = (f32[512]{0:T(512)S(1)}, f32[512,1024]{1,0:T(8,128)}) fusion(bf16[512,1024]{1,0:T(8,128)(2,1)S(1)} %copy-done.4, pred[512]{0:T(512)(128)(4,1)S(1)} %get-tuple-element.3, bf16[512,4096]{1,0:T(8,128)(2,1)} %copy-done.2, bf16[4096,1024]{1,0:T(8,128)(2,1)} %all-gather.14.cloned.1.call-done), kind=kOutput, calls=%fused_computation.14 | convolution fusion | flops 4297588224 | bytes 15731200 | tf_op jit(solution)/shard_map/dot_general | solution.py:91
  784.3 21.3 %psum.15 = f32[512]{0:T(512)S(1)} all-reduce(f32[512]{0:T(512)S(1)} %get-tuple-element.7), channel_id=1, replica_groups=mesh['dp'=4,'tensor'=8] {'tensor'}, use_global_device_ids=true, to_apply=%region_8.9 | all-reduce | flops 512 | bytes 4096 | tf_op jit(solution)/shard_map/psum | solution.py:96
  (48 shorter events, 10.4 us)
Async XLA Ops:
  7.2 2.9 copy-start
  7.2 80.2 %all-gather.6.cloned.1.call-start = ((), (), s32[]{:S(2)}) async-start(), calls=%async_computation.3 | async-start | bytes 4718592 | tf_op jit(solution)/shard_map/all_gather | solution.py:69
  7.9 173.3 %all-gather.8.cloned.1.call-start = ((), (), s32[]{:S(2)}) async-start(), calls=%async_computation.4 | async-start | bytes 18350080 | tf_op jit(solution)/shard_map/all_gather | solution.py:79
  8.7 268.1 %all-gather.12.cloned.1.call-start = ((), (), s32[]{:S(2)}) async-start(), calls=%async_computation.6 | async-start | bytes 18350080 | tf_op jit(solution)/shard_map/all_gather | solution.py:83
  9.4 362.8 %all-gather.10.cloned.1.call-start = ((), (), s32[]{:S(2)}) async-start(), calls=%async_computation.5 | async-start | bytes 18350080 | tf_op jit(solution)/shard_map/all_gather | solution.py:80
  10.0 513.2 %reduce-scatter.2.cloned.1.call-start = ((), (), s32[]{:S(2)}) async-start(), calls=%async_computation.9 | async-start | bytes 9437184 | tf_op jit(solution)/shard_map/reduce_scatter | solution.py:27
  26.8 0.7 copy-start.6
  26.8 688.0 %all-reduce.2.cloned.1.call-start = ((), (), s32[]{:S(2)}) async-start(), calls=%async_computation.7 | async-start | bytes 8388608 | tf_op jit(solution)/shard_map/psum | solution.py:86
  401.0 0.8 copy-start.5
  401.0 0.8 copy-start.7
  401.0 122.2 %copy-start.3 = (bf16[64,8192]{1,0:T(8,128)(2,1)S(1)}, bf16[64,8192]{1,0:T(8,128)(2,1)}, u32[]{:S(2)}) copy-start(bf16[64,8192]{1,0:T(8,128)(2,1)} %param.13) | copy-start | bytes 3145732
  401.0 372.7 %all-gather.14.cloned.1.call-start = ((), (), s32[]{:S(2)}) async-start(), calls=%async_computation.8 | async-start | bytes 10485760 | tf_op jit(solution)/shard_map/all_gather | solution.py:92
  559.1 77.3 %all-to-all-start.1 = ((bf16[4,8,32,1024]{3,2,0,1:T(8,128)(2,1)}), bf16[4,8,32,1024]{3,2,0,1:T(8,128)(2,1)}, u32[]{:S(2)}, u32[]{:S(2)}) async-start(bf16[4,8,32,1024]{3,2,0,1:T(8,128)(2,1)} %copy.33), calls=%async_computation.2 | async-start | bytes 4194304 | tf_op jit(solution)/shard_map/all_to_all | solution.py:57
  641.1 132.7 %copy-start.4 = (bf16[512,1024]{1,0:T(8,128)(2,1)S(1)}, bf16[512,1024]{1,0:T(8,128)(2,1)}, u32[]{:S(2)}) copy-start(bf16[512,1024]{1,0:T(8,128)(2,1)} %gather_fusion) | copy-start | bytes 3145732
  719.9 2.0 copy-start.2
  773.7 32.5 %copy-start.1 = (bf16[512,1024]{1,0:T(8,128)(2,1)S(1)}, bf16[512,1024]{1,0:T(8,128)(2,1)}, u32[]{:S(2)}) copy-start(bf16[512,1024]{1,0:T(8,128)(2,1)} %param.11) | copy-start | bytes 3145732
Sparse Core Ops, SparseCore 0:
  10.0 77.3 all-gather.5
  89.0 92.1 all-gather.7
  182.8 93.9 all-gather.11
  278.2 93.9 all-gather.9
  375.7 147.4 reduce-scatter.1
  526.7 188.0 all-reduce.1
  716.4 57.2 all-gather.13
where the time goes:
time: 814 us; the launch traced here: 813 us
  waiting for transfers between devices  639 us (79%)
  matrix products  72.8 us (9%)
  blocking collectives  49.5 us (6%)
  local copies, waits for them, and re-layouts  20.5 us (3%)
  between operations  14.3 us (2%)
  other arithmetic  12.4 us (2%)
    reduce_scatter x1, waiting for transfers between devices, local(): lax.psum_scatter(jnp.dot(portion, w_out, preferred_element_type=jnp.float...  119 us
    all_gather x1, waiting for transfers between devices, local(): up_acts = add_rows(lax.all_gather(w_up, 'dp', axis=0, tiled=True))  95.4 us
    all_gather x1, waiting for transfers between devices, local(): gate_acts = add_rows(lax.all_gather(w_gate, 'dp', axis=0, tiled=True))  90.7 us
    all_gather x1, waiting for transfers between devices, local(): lax.all_gather(w_down, 'dp', axis=1, tiled=True)  80.9 us
    psum x1, waiting for transfers between devices, local(): lax.psum(partial_sum.astype(jnp.bfloat16), 'tensor').astype(jnp.float32)  73.8 us
    all_to_all x1, waiting for transfers between devices, local(): lax.all_to_all(lax.all_to_all(send_blocks, 'dp', split_axis=0, concat_axi...  64.3 us
    all_gather x1, waiting for transfers between devices, local(): gathered = lax.all_gather(student_in, 'tensor', axis=1, tiled=True)  59.9 us
    all_gather x1, waiting for transfers between devices, local(): lax.all_gather(proj, 'dp', axis=0, tiled=True)  51 us
  transfers between devices with their start and end apart: 8, of which 8 were waited for; matrix products, arithmetic and copies ran while one was open for 11% of the time, Pallas kernels for 0%

commit v1 on v0

--- a/solution.py
+++ b/solution.py
@@ -66,7 +66,14 @@
     inverse = jnp.zeros(dest_row.shape, jnp.int32).at[dest_row].set(arrival_index)
     own_arrivals = lax.dynamic_slice_in_dim(inverse, lax.axis_index("dp") * tile_rows, tile_rows, 0)
     target = jnp.take(flattened, own_arrivals, axis=0)
-    gathered = lax.all_gather(student_in, "tensor", axis=1, tiled=True)
+    ring = [student_in]
+    for hop in range(7):
+        ring.append(lax.ppermute(ring[-1], "tensor", [(dev, (dev + 1) % 8) for dev in range(8)]))
+    gathered = jnp.roll(
+        jnp.concatenate(ring[::-1], axis=1),
+        (lax.axis_index("tensor") + 1) * ring[0].shape[1],
+        axis=1,
+    )
     x_full = gathered.astype(jnp.float32)
     student_mean = jnp.mean(x_full * x_full, axis=1, keepdims=True)
     normed = (x_full * lax.rsqrt(student_mean + 1e-05) * student_gain.astype(jnp.float32)).astype(

time: 814 us -> 562 us (0.69)
  waiting for transfers between devices: 639 us -> 350 us
  blocking collectives: 49.5 us -> 70.1 us
  local copies, waits for them, and re-layouts: 20.5 us -> 30.9 us
    reduce_scatter x1, waiting for transfers between devices: 119 us -> 0.03 us  [local(): lax.psum_scatter(jnp.dot(portion, w_out, preferred_element_type=jnp.float...]
    all_gather x1, waiting for transfers between devices: 90.7 us -> 0.02 us  [local(): gate_acts = add_rows(lax.all_gather(w_gate, 'dp', axis=0, tiled=True))]
    ppermute x0 -> x7, waiting for transfers between devices: none -> 85.4 us  [local(): lax.ppermute(ring[-1], 'tensor', [(dev, (dev + 1) % 8) for dev in range(8)])]
    all_gather x1 -> x0, waiting for transfers between devices: 59.9 us -> none  [local(): gathered = lax.all_gather(student_in, 'tensor', axis=1, tiled=True)]
    all_gather x1, waiting for transfers between devices: 51 us -> 0.01 us  [local(): lax.all_gather(proj, 'dp', axis=0, tiled=True)]
    all_gather x1, waiting for transfers between devices: 95.4 us -> 59.3 us  [local(): up_acts = add_rows(lax.all_gather(w_up, 'dp', axis=0, tiled=True))]
    psum x1, waiting for transfers between devices: 73.8 us -> 49.9 us  [local(): lax.psum(partial_sum.astype(jnp.bfloat16), 'tensor').astype(jnp.float32)]
    all_to_all x1, blocking collectives: 28.2 us -> 51 us  [local(): lax.all_to_all(send_blocks, 'dp', split_axis=0, concat_axis=0, tiled=True)]
  transfers between devices with their start and end apart: 8 -> 14, of which waited for: 8 -> 10; matrix products, arithmetic and copies ran while one was open for 11% -> 17% of each run, Pallas kernels for 0% -> 0%
where the time goes in v1:
time: 562 us; the launch traced here: 561 us
  waiting for transfers between devices  350 us (62%)
  matrix products  73 us (13%)
  blocking collectives  70.1 us (12%)
  local copies, waits for them, and re-layouts  30.9 us (5%)
  between operations  15.5 us (3%)
  other arithmetic  12.4 us (2%)
  starting transfers between devices  9.08 us (2%)
    all_gather x1, waiting for transfers between devices, local(): lax.all_gather(w_down, 'dp', axis=1, tiled=True)  95.6 us
    ppermute x7, waiting for transfers between devices, local(): lax.ppermute(ring[-1], 'tensor', [(dev, (dev + 1) % 8) for dev in range(8)])  85.4 us
    all_gather x1, waiting for transfers between devices, local(): up_acts = add_rows(lax.all_gather(w_up, 'dp', axis=0, tiled=True))  59.3 us
    all_to_all x1, waiting for transfers between devices, local(): lax.all_to_all(lax.all_to_all(send_blocks, 'dp', split_axis=0, concat_axi...  57.3 us
    all_to_all x1, blocking collectives, local(): lax.all_to_all(send_blocks, 'dp', split_axis=0, concat_axis=0, tiled=True)  51 us
    psum x1, waiting for transfers between devices, local(): lax.psum(partial_sum.astype(jnp.bfloat16), 'tensor').astype(jnp.float32)  49.9 us
    dot_general x1, matrix products, local(): jnp.dot(hidden, lax.all_gather(w_down, 'dp', axis=1, tiled=True), preferr...  28.8 us
    psum x1, blocking collectives, local(): row_loss = lax.psum(row_error, 'tensor') / HT  19.1 us
  transfers between devices with their start and end apart: 14, of which 10 were waited for; matrix products, arithmetic and copies ran while one was open for 17% of the time, Pallas kernels for 0%

profile of v1, /device:TPU:0, one launch (start us, length us, event | category | flops | bytes accessed | tf_op | source)
XLA Modules:
  0.0 561.0 jit_solution(1530038092957225088)
XLA Ops:
  10.3 3.0 collective-permute-start
  13.4 15.0 %collective-permute-done = bf16[512,512]{1,0:T(8,128)(2,1)S(1)} collective-permute-done((bf16[512,512]{1,0:T(8,128)(2,1)S(1)}, bf16[512,512]{1,0:T(8,128)(2,1)S(1)}, u32[]{:S(2)}, u32[]{:S(2)}) %collective-permute-start) | collective-permute-done | bytes 524320 | tf_op jit(solution)/shard_map/ppermute | solution.py:71
  28.3 15.8 %collective-permute-done.1 = bf16[512,512]{1,0:T(8,128)(2,1)S(1)} collective-permute-done((bf16[512,512]{1,0:T(8,128)(2,1)S(1)}, bf16[512,512]{1,0:T(8,128)(2,1)S(1)}, u32[]{:S(2)}, u32[]{:S(2)}) %collective-permute-start.1) | collective-permute-done | bytes 524320 | tf_op jit(solution)/shard_map/ppermute | solution.py:71
  44.1 14.9 %collective-permute-done.2 = bf16[512,512]{1,0:T(8,128)(2,1)S(1)} collective-permute-done((bf16[512,512]{1,0:T(8,128)(2,1)S(1)}, bf16[512,512]{1,0:T(8,128)(2,1)S(1)}, u32[]{:S(2)}, u32[]{:S(2)}) %collective-permute-start.2) | collective-permute-done | bytes 524320 | tf_op jit(solution)/shard_map/ppermute | solution.py:71
  59.0 14.1 %collective-permute-done.3 = bf16[512,512]{1,0:T(8,128)(2,1)S(1)} collective-permute-done((bf16[512,512]{1,0:T(8,128)(2,1)S(1)}, bf16[512,512]{1,0:T(8,128)(2,1)S(1)}, u32[]{:S(2)}, u32[]{:S(2)}) %collective-permute-start.3) | collective-permute-done | bytes 524320 | tf_op jit(solution)/shard_map/ppermute | solution.py:71
  73.9 13.2 %collective-permute-done.4 = bf16[512,512]{1,0:T(8,128)(2,1)S(1)} collective-permute-done((bf16[512,512]{1,0:T(8,128)(2,1)S(1)}, bf16[512,512]{1,0:T(8,128)(2,1)S(1)}, u32[]{:S(2)}, u32[]{:S(2)}) %collective-permute-start.4) | collective-permute-done | bytes 524320 | tf_op jit(solution)/shard_map/ppermute | solution.py:71
  87.9 12.5 %collective-permute-done.5 = bf16[512,512]{1,0:T(8,128)(2,1)} collective-permute-done((bf16[512,512]{1,0:T(8,128)(2,1)S(1)}, bf16[512,512]{1,0:T(8,128)(2,1)}, u32[]{:S(2)}, u32[]{:S(2)}) %collective-permute-start.5) | collective-permute-done | bytes 524320 | tf_op jit(solution)/shard_map/ppermute | solution.py:71
  100.4 16.8 %convolution_convert_fusion = bf16[512,8192]{1,0:T(8,128)(2,1)} fusion(bf16[512,1024]{1,0:T(8,128)(2,1)S(1)} %copy-done, bf16[1024,8192]{1,0:T(8,128)(2,1)} %param.12), kind=kOutput, calls=%fused_computation.5 | convolution fusion | flops 8594128896 | bytes 26214400 | tf_op jit(solution)/shard_map/dot_general | solution.py:28
  123.8 4.1 copy-done.2
  128.8 14.6 %fusion.13 = f32[512,1792]{1,0:T(8,128)} fusion(bf16[4096,1792]{1,0:T(8,128)(2,1)} %all-gather.5.cloned.1.call-done, f32[4096]{0:T(1024)S(1)} %convert_element_type.47, f32[512]{0:T(512)S(1)} %add_rsqrt_fusion, bf16[512,8192]{1,0:T(8,128)(2,1)} %copy-done.2, s32[]{:T(128)S(6)} %select_n.42), kind=kOutput, calls=%fused_computation.27 | convolution fusion | flops 7524581376 | bytes 22562820 | tf_op jit(solution)/shard_map/dot_general | solution.py:84
  143.4 59.3 %all-gather.7.cloned.1.call-done = bf16[4096,1792]{1,0:T(8,128)(2,1)} async-done(((bf16[1024,1792]{1,0:T(8,128)(2,1)}), bf16[4096,1792]{1,0:T(8,128)(2,1)}) %all-gather.7.cloned.1.call-update) | async-done | bytes 14680080 | tf_op jit(solution)/shard_map/all_gather | solution.py:87
  202.7 95.6 %all-gather.9.cloned.1.call-done = bf16[1792,4096]{1,0:T(8,128)(2,1)} async-done(((bf16[1792,1024]{1,0:T(8,128)(2,1)}), bf16[1792,4096]{1,0:T(8,128)(2,1)}) %all-gather.9.cloned.1.call-update) | async-done | bytes 14680080 | tf_op jit(solution)/shard_map/all_gather | solution.py:90
  298.3 28.8 %convolution_convert_fusion.2 = bf16[512,4096]{1,0:T(8,128)(2,1)} fusion(bf16[1792,4096]{1,0:T(8,128)(2,1)} %all-gather.9.cloned.1.call-done, f32[512,1792]{1,0:T(8,128)} %fusion.13, bf16[4096,1792]{1,0:T(8,128)(2,1)} %all-gather.7.cloned.1.call-done, f32[4096]{0:T(1024)S(1)} %convert_element_type.47, f32[512]{0:T(512)S(1)} %add_rsqrt_fusion, ...), kind=kOutput, calls=%fused_computation.11 | convolution fusion | flops 15048376320 | bytes 41437188 | tf_op jit(solution)/shard_map/dot_general | solution.py:89
  331.6 2.1 convolution_convert_fusion.1
  336.3 51.0 %all_to_all.10 = bf16[4,8,32,1024]{3,2,1,0:T(8,128)(2,1)S(1)} all-to-all(bf16[4,8,32,1024]{3,2,1,0:T(8,128)(2,1)S(1)} %bitcast.17), channel_id=1, replica_groups=mesh['dp'=4,'tensor'=8] {'dp'}, dimensions={0} | all-to-all | bytes 4194304 | tf_op jit(solution)/shard_map/all_to_all | solution.py:58
  388.7 5.4 all-to-all-start.1
  394.3 8.3 %scatter_custom_fusion = s32[2048]{0:T(1024)S(1)} fusion(s32[2048]{0:T(1024)S(1)} %get-tuple-element.5, s32[2048]{0:T(1024)S(1)} %reshape.60, s32[]{:T(128)} %constant.77.clone.1), kind=kCustom, calls=%fused_computation.59 | custom fusion | bytes 8196 | tf_op jit(solution)/shard_map/scatter | solution.py:66
  402.7 57.3 %all-to-all-done.1 = bf16[4,8,32,1024]{3,2,0,1:T(8,128)(2,1)} async-done(((bf16[4,8,32,1024]{3,2,0,1:T(8,128)(2,1)}), bf16[4,8,32,1024]{3,2,0,1:T(8,128)(2,1)}, u32[]{:S(2)}, u32[]{:S(2)}) %all-to-all-start.1) | async-done | bytes 2097184 | tf_op jit(solution)/shard_map/all_to_all | solution.py:57
  461.8 2.8 gather_fusion
  464.6 49.9 %all-reduce.2.cloned.1.call-done = bf16[512,4096]{1,0:T(8,128)(2,1)} async-done(((bf16[512,4096]{1,0:T(8,128)(2,1)}), bf16[512,4096]{1,0:T(8,128)(2,1)}) %all-reduce.2.cloned.1.call-update) | async-done | bytes 4194320 | tf_op jit(solution)/shard_map/psum | solution.py:93
  514.5 7.2 %fusion.3 = bf16[512,4096]{1,0:T(8,128)(2,1)} fusion(bf16[512,4096]{1,0:T(8,128)(2,1)} %all-reduce.2.cloned.1.call-done, bf16[512,8192]{1,0:T(8,128)(2,1)} %copy-done.2, s32[]{:T(128)S(6)} %select_n.42), kind=kLoop, calls=%fused_computation.10 | loop fusion | flops 8388608 | bytes 12582916 | tf_op jit(solution)/shard_map/convert_element_type | solution.py:94
  521.7 10.6 %multiply_reduce_fusion = (f32[512]{0:T(512)S(1)}, f32[512,1024]{1,0:T(8,128)}) fusion(bf16[512,1024]{1,0:T(8,128)(2,1)S(1)} %copy-done.9, pred[512]{0:T(512)(128)(4,1)S(1)} %get-tuple-element.3, bf16[512,4096]{1,0:T(8,128)(2,1)} %fusion.3, bf16[4096,1024]{1,0:T(8,128)(2,1)} %all-gather.11.cloned.1.call-done), kind=kOutput, calls=%fused_computation.14 | convolution fusion | flops 4297588224 | bytes 15731200 | tf_op jit(solution)/shard_map/dot_general | solution.py:98
  532.3 19.1 %psum.15 = f32[512]{0:T(512)S(1)} all-reduce(f32[512]{0:T(512)S(1)} %get-tuple-element.7), channel_id=1, replica_groups=mesh['dp'=4,'tensor'=8] {'tensor'}, use_global_device_ids=true, to_apply=%region_8.9 | all-reduce | flops 512 | bytes 4096 | tf_op jit(solution)/shard_map/psum | solution.py:103
  552.0 1.9 constant_dynamic-slice_fusion
  (85 shorter events, 22.3 us)
Async XLA Ops:
  8.0 92.4 %copy-start = (bf16[512,1024]{1,0:T(8,128)(2,1)S(1)}, bf16[512,1024]{1,0:T(8,128)(2,1)}, u32[]{:S(2)}) copy-start(bf16[512,1024]{1,0:T(8,128)(2,1)} %param.11) | copy-start | bytes 3145732
  8.0 2.3 copy-start.4
  8.0 120.8 %all-gather.5.cloned.1.call-start = ((), (), s32[]{:S(2)}) async-start(), calls=%async_computation.3 | async-start | bytes 18350080 | tf_op jit(solution)/shard_map/all_gather | solution.py:86
  8.8 194.0 %all-gather.7.cloned.1.call-start = ((), (), s32[]{:S(2)}) async-start(), calls=%async_computation.4 | async-start | bytes 18350080 | tf_op jit(solution)/shard_map/all_gather | solution.py:87
  9.5 288.8 %all-gather.9.cloned.1.call-start = ((), (), s32[]{:S(2)}) async-start(), calls=%async_computation.5 | async-start | bytes 18350080 | tf_op jit(solution)/shard_map/all_gather | solution.py:90
  10.2 319.6 %reduce-scatter.2.cloned.1.call-start = ((), (), s32[]{:S(2)}) async-start(), calls=%async_computation.8 | async-start | bytes 9437184 | tf_op jit(solution)/shard_map/reduce_scatter | solution.py:27
  10.3 18.0 %collective-permute-start = (bf16[512,512]{1,0:T(8,128)(2,1)S(1)}, bf16[512,512]{1,0:T(8,128)(2,1)S(1)}, u32[]{:S(2)}, u32[]{:S(2)}) collective-permute-start(bf16[512,512]{1,0:T(8,128)(2,1)S(1)} %copy-done.4), channel_id=1, source_target_pairs={{0,1},{1,2},{2,3},{3,4},{4,5},{5,6},{6,7},{7,0},{8,9},{9,10},{10,1... | collective-permute-start | bytes 1572872 | tf_op jit(solution)/shard_map/ppermute | solution.py:71
  28.3 15.8 %collective-permute-start.1 = (bf16[512,512]{1,0:T(8,128)(2,1)S(1)}, bf16[512,512]{1,0:T(8,128)(2,1)S(1)}, u32[]{:S(2)}, u32[]{:S(2)}) collective-permute-start(bf16[512,512]{1,0:T(8,128)(2,1)S(1)} %collective-permute-done), channel_id=1, source_target_pairs={{0,1},{1,2},{2,3},{3,4},{4,5},{5,6},{6,7},{7,0},{8,9},{9,10},{10,1... | collective-permute-start | bytes 1572872 | tf_op jit(solution)/shard_map/ppermute | solution.py:71
  44.1 14.9 %collective-permute-start.2 = (bf16[512,512]{1,0:T(8,128)(2,1)S(1)}, bf16[512,512]{1,0:T(8,128)(2,1)S(1)}, u32[]{:S(2)}, u32[]{:S(2)}) collective-permute-start(bf16[512,512]{1,0:T(8,128)(2,1)S(1)} %collective-permute-done.1), channel_id=1, source_target_pairs={{0,1},{1,2},{2,3},{3,4},{4,5},{5,6},{6,7},{7,0},{8,9},{9,10},{10,1... | collective-permute-start | bytes 1572872 | tf_op jit(solution)/shard_map/ppermute | solution.py:71
  59.0 14.1 %collective-permute-start.3 = (bf16[512,512]{1,0:T(8,128)(2,1)S(1)}, bf16[512,512]{1,0:T(8,128)(2,1)S(1)}, u32[]{:S(2)}, u32[]{:S(2)}) collective-permute-start(bf16[512,512]{1,0:T(8,128)(2,1)S(1)} %collective-permute-done.2), channel_id=1, source_target_pairs={{0,1},{1,2},{2,3},{3,4},{4,5},{5,6},{6,7},{7,0},{8,9},{9,10},{10,1... | collective-permute-start | bytes 1572872 | tf_op jit(solution)/shard_map/ppermute | solution.py:71
  73.9 13.2 %collective-permute-start.4 = (bf16[512,512]{1,0:T(8,128)(2,1)S(1)}, bf16[512,512]{1,0:T(8,128)(2,1)S(1)}, u32[]{:S(2)}, u32[]{:S(2)}) collective-permute-start(bf16[512,512]{1,0:T(8,128)(2,1)S(1)} %collective-permute-done.3), channel_id=1, source_target_pairs={{0,1},{1,2},{2,3},{3,4},{4,5},{5,6},{6,7},{7,0},{8,9},{9,10},{10,1... | collective-permute-start | bytes 1572872 | tf_op jit(solution)/shard_map/ppermute | solution.py:71
  87.9 12.5 %collective-permute-start.5 = (bf16[512,512]{1,0:T(8,128)(2,1)S(1)}, bf16[512,512]{1,0:T(8,128)(2,1)}, u32[]{:S(2)}, u32[]{:S(2)}) collective-permute-start(bf16[512,512]{1,0:T(8,128)(2,1)S(1)} %collective-permute-done.4), channel_id=1, source_target_pairs={{0,1},{1,2},{2,3},{3,4},{4,5},{5,6},{6,7},{7,0},{8,9},{9,10},{10,1... | collective-permute-start | bytes 1572872 | tf_op jit(solution)/shard_map/ppermute | solution.py:71
  100.4 17.6 %collective-permute-start.6 = (bf16[512,512]{1,0:T(8,128)(2,1)}, bf16[512,512]{1,0:T(8,128)(2,1)}, u32[]{:S(2)}, u32[]{:S(2)}) collective-permute-start(bf16[512,512]{1,0:T(8,128)(2,1)} %collective-permute-done.5), channel_id=1, source_target_pairs={{0,1},{1,2},{2,3},{3,4},{4,5},{5,6},{6,7},{7,0},{8,9},{9,10},{10,1... | collective-permute-start | bytes 1572872 | tf_op jit(solution)/shard_map/ppermute | solution.py:71
  117.2 3.2 copy-start.8
  117.2 3.3 copy-start.6
  117.3 397.2 %all-reduce.2.cloned.1.call-start = ((), (), s32[]{:S(2)}) async-start(), calls=%async_computation.6 | async-start | bytes 8388608 | tf_op jit(solution)/shard_map/psum | solution.py:93
  123.8 4.1 copy-start.2
  298.3 29.4 %copy-start.12 = (s32[2048]{0:T(1024)S(1)}, s32[2048]{0:T(1024)}, u32[]{:S(2)}) copy-start(s32[2048]{0:T(1024)} %param.15) | copy-start | bytes 24580
  298.3 29.6 %copy-start.10 = (bf16[8192]{0:T(1024)(128)(2,1)S(1)}, bf16[8192]{0:T(1024)(128)(2,1)}, u32[]{:S(2)}) copy-start(bf16[8192]{0:T(1024)(128)(2,1)} %param.14) | copy-start | bytes 49156
  298.3 31.6 %copy-start.3 = (bf16[64,8192]{1,0:T(8,128)(2,1)S(1)}, bf16[64,8192]{1,0:T(8,128)(2,1)}, u32[]{:S(2)}) copy-start(bf16[64,8192]{1,0:T(8,128)(2,1)} %param.13) | copy-start | bytes 3145732
  327.2 194.5 %all-gather.11.cloned.1.call-start = ((), (), s32[]{:S(2)}) async-start(), calls=%async_computation.7 | async-start | bytes 10485760 | tf_op jit(solution)/shard_map/all_gather | solution.py:99
  388.7 71.3 %all-to-all-start.1 = ((bf16[4,8,32,1024]{3,2,0,1:T(8,128)(2,1)}), bf16[4,8,32,1024]{3,2,0,1:T(8,128)(2,1)}, u32[]{:S(2)}, u32[]{:S(2)}) async-start(bf16[4,8,32,1024]{3,2,0,1:T(8,128)(2,1)} %copy.33), calls=%async_computation.2 | async-start | bytes 4194304 | tf_op jit(solution)/shard_map/all_to_all | solution.py:57
  464.6 57.1 %copy-start.9 = (bf16[512,1024]{1,0:T(8,128)(2,1)S(1)}, bf16[512,1024]{1,0:T(8,128)(2,1)}, u32[]{:S(2)}) copy-start(bf16[512,1024]{1,0:T(8,128)(2,1)} %gather_fusion) | copy-start | bytes 3145732
  521.7 32.2 %copy-start.1 = (bf16[512,1024]{1,0:T(8,128)(2,1)S(1)}, bf16[512,1024]{1,0:T(8,128)(2,1)}, u32[]{:S(2)}) copy-start(bf16[512,1024]{1,0:T(8,128)(2,1)} %param.11) | copy-start | bytes 3145732
  (3 other events, 2.3 us)
Sparse Core Ops, SparseCore 0:
  10.4 96.6 all-gather.4
  108.7 93.9 all-gather.6
  204.3 93.9 all-gather.8
  329.2 80.7 all-gather.10
Sparse Core Ops, SparseCore 1:
  117.3 148.0 reduce-scatter.1
  327.2 187.2 all-reduce.1
